TPU v7x, 32 devices: a whole 2x2x4 slice. The times are simulated.
32 devices in a mesh: slab: 8 (over y, x, core), col: 4 (over z).
Axes of the slice: x: 2, y: 2, z: 4, core: 2. Of those that a mesh axis runs over, the one named last changes fastest.
Arguments:
- hamiltonian_blocks: bfloat16 [128, 9, 128, 128], P('slab'), may hold values from -0.0625 to 0.0625
- block_columns: int32 [128, 9], P('slab'), may hold values from 0 to 127, as said below
- probe: bfloat16 [16384, 2048], P('slab', 'col'), may hold values from -6 to 6
- previous: float32 [16384, 2048], P('slab', 'col'), may hold values from -6 to 6
- current: float32 [16384, 2048], P('slab', 'col'), may hold values from -6 to 6
- orbital_weight: float32 [16384], P('slab'), may hold values from 0.1 to 10
Outputs:
- last_previous: float32 [16384, 2048], P('slab', 'col')
- last_current: float32 [16384, 2048], P('slab', 'col')
- moments: float32 [3, 2048], P(None, 'col')
Inputs may be any that keep to these rules, and one draw needn't show every extreme that they name: `block_columns`: the 9 entries of a row are distinct block columns within 5 of the row's own block row, counted cyclically modulo 128; they include the row itself and the block rows 5 before and 5 after it.
All inputs are finite; a program needn't handle non-finite values.
Results may differ from a plain program's by a relative error of at most 0.0024.
Values may be sent and summed in bfloat16 or wider, within the bound.
A program may use at most 192 MiB of HBM per device.

v0:
```python
import functools

import jax
import jax.numpy as jnp
from jax import lax
from jax.experimental import pallas as pl
from jax.experimental.pallas import tpu as pltpu
from jax.sharding import PartitionSpec as P

BAND = 5
TERMS = 3
LANES = 128
CHUNK = 256
GROUP = 2


def kernel(
    n, col_ref, ow_ref, h_hbm, probe_hbm, prev_hbm, cur_hbm,
    last_prev, last_cur, mom_ref,
    hv, hb, ext, tb, wts, pv, mom,
    in_sem, out_sem, send_sem, recv_sem, msend, mrecv,
):
    me = lax.axis_index("slab")
    rows, slots, w, _ = hv.shape
    chunks, height, cc = wts.shape
    total = n * rows
    rim = BAND * w
    gw = GROUP * w
    pairs = rows // GROUP
    edge = -(-BAND // GROUP)
    depth = gw + 2 * rim
    first = me * rows
    low, high = lax.rem(me + n - 1, n), lax.rem(me + 1, n)

    def columns(c):
        return pl.ds(c * cc, cc)

    pieces = ((0, rim), (height - rim, rim), (rim, height - 2 * rim))
    cur_in = {}
    for c in range(chunks):
        for k, (start, size) in enumerate(pieces):
            cur_in[c, k] = pltpu.make_async_copy(
                cur_hbm.at[pl.ds(start, size), columns(c)],
                tb.at[1, c, pl.ds(start, size)],
                in_sem.at[3 * c + k],
            )
    base = 3 * chunks
    h_in = pltpu.make_async_copy(h_hbm, hv, in_sem.at[base])
    probe_in = pltpu.make_async_copy(probe_hbm, pv, in_sem.at[base + 1])
    prev_in = [
        pltpu.make_async_copy(prev_hbm.at[:, columns(c)], tb.at[0, c], in_sem.at[base + 2 + c])
        for c in range(chunks)
    ]
    for c in range(chunks):
        cur_in[c, 0].start()
        cur_in[c, 1].start()

    barrier = pltpu.get_barrier_semaphore()
    for k in range(1, n):
        pl.semaphore_signal(
            barrier, inc=1, device_id={"slab": lax.rem(me + k, n)},
            device_id_type=pl.DeviceIdType.MESH,
        )

    def halo(t, c):
        down = pltpu.make_async_remote_copy(
            src_ref=ext.at[t, c, pl.ds(rim, rim)],
            dst_ref=ext.at[t, c, pl.ds(rim + height, rim)],
            send_sem=send_sem.at[t, c, 0], recv_sem=recv_sem.at[t, c, 0],
            device_id={"slab": low}, device_id_type=pl.DeviceIdType.MESH,
        )
        up = pltpu.make_async_remote_copy(
            src_ref=ext.at[t, c, pl.ds(height, rim)],
            dst_ref=ext.at[t, c, pl.ds(0, rim)],
            send_sem=send_sem.at[t, c, 1], recv_sem=recv_sem.at[t, c, 1],
            device_id={"slab": high}, device_id_type=pl.DeviceIdType.MESH,
        )
        return down, up

    def cast(c, k):
        start, size = pieces[k]
        steps = size // w

        def body(i, carry):
            at = pl.multiple_of(start + i * w, w)
            ext[0, c, pl.ds(pl.multiple_of(rim + at, w), w)] = tb[1, c, pl.ds(at, w)].astype(jnp.bfloat16)
            return carry

        lax.fori_loop(0, steps, body, 0)

    halos = {(t, c): halo(t, c) for t in range(TERMS) for c in range(chunks)}
    for c in range(chunks):
        cur_in[c, 0].wait()
        cur_in[c, 1].wait()
        if c == 0:
            for k in range(chunks):
                cur_in[k, 2].start()
            h_in.start()
            probe_in.start()
            for copy in prev_in:
                copy.start()
        cast(c, 0)
        cast(c, 1)
        if c == 0:
            pl.semaphore_wait(barrier, n - 1)
        for copy in halos[0, c]:
            copy.start()
    for c in range(chunks):
        cur_in[c, 2].wait()
        cast(c, 2)

    h_in.wait()
    zero = jnp.zeros((w, w), jnp.bfloat16)

    def build(p, carry):
        for half in range(GROUP):
            r = p * GROUP + half
            places = []
            for s in range(slots):
                x = col_ref[r, s] - (first + r) + BAND
                x = jnp.where(x < 0, x + total, x)
                places.append(jnp.where(x >= total, x - total, x))
            for d in range(GROUP + 2 * BAND):
                place = d - half
                if place < 0 or place > 2 * BAND:
                    block = zero
                else:
                    slot = jnp.int32(0)
                    hit = jnp.int32(0)
                    for s in range(slots):
                        same = places[s] == place
                        slot = jnp.where(same, s, slot)
                        hit = jnp.where(same, 1, hit)
                    block = jnp.where(hit == 1, hv[r, slot], zero)
                hb[p, half * w:(half + 1) * w, d * w:(d + 1) * w] = block
        return carry

    lax.fori_loop(0, pairs, build, 0)

    probe_in.wait()
    eye = lax.broadcasted_iota(jnp.int32, (w, w), 0) == lax.broadcasted_iota(jnp.int32, (w, w), 1)

    def weigh(r, carry):
        row = jnp.broadcast_to(ow_ref[pl.ds(r, 1), :], (w, w))
        column = jnp.sum(jnp.where(eye, row, 0.0), axis=1, keepdims=True) / (total * w)
        at = pl.multiple_of(r * w, w)
        for c in range(chunks):
            wts[c, pl.ds(at, w)] = column * pv[pl.ds(at, w), c * cc:(c + 1) * cc].astype(jnp.float32)
        return carry

    lax.fori_loop(0, rows, weigh, 0)
    for copy in prev_in:
        copy.wait()

    def tile(t, c, p, acc):
        at = pl.multiple_of(p * gw, gw)
        product = jnp.dot(hb[p], ext[t, c, pl.ds(at, depth)], preferred_element_type=jnp.float32)
        upcoming = 2.0 * product - tb[t % 2, c, pl.ds(at, gw)]
        tb[t % 2, c, pl.ds(at, gw)] = upcoming
        if t + 1 < TERMS:
            ext[t + 1, c, pl.ds(pl.multiple_of(rim + at, w), gw)] = upcoming.astype(jnp.bfloat16)
        y = wts[c, pl.ds(at, gw)] * upcoming
        return acc + jnp.sum(y.reshape(gw // 8, 8, cc), axis=0)

    def sums(t):
        return [
            pltpu.make_async_remote_copy(
                src_ref=mom.at[t, me], dst_ref=mom.at[t, me],
                send_sem=msend.at[t, k], recv_sem=mrecv.at[t, k],
                device_id={"slab": lax.rem(me + k, n)}, device_id_type=pl.DeviceIdType.MESH,
            )
            for k in range(1, n)
        ]

    outs = []
    sent = []
    mid_at, mid_size = edge * gw, height - 2 * edge * gw
    for t in range(TERMS):
        for c in range(chunks):
            acc = jnp.zeros((8, cc), jnp.float32)
            acc = lax.fori_loop(edge, pairs - edge, lambda p, a: tile(t, c, p, a), acc)
            for copy in halos[t, c]:
                copy.wait()
            if t == TERMS - 1:
                copy = pltpu.make_async_copy(
                    tb.at[t % 2, c, pl.ds(mid_at, mid_size)],
                    last_cur.at[pl.ds(mid_at, mid_size), columns(c)], out_sem.at[c, 0])
                copy.start()
                outs.append(copy)
            acc = lax.fori_loop(
                0, 2 * edge,
                lambda i, a: tile(t, c, jnp.where(i < edge, i, i + (pairs - 2 * edge)), a), acc)
            if t + 1 < TERMS:
                for copy in halos[t + 1, c]:
                    copy.start()
            total_row = jnp.sum(acc, axis=0, keepdims=True)
            for k in range(cc // LANES):
                mom[t, me, pl.ds(c * (cc // LANES) + k, 1), :] = total_row[:, k * LANES:(k + 1) * LANES]
            if t == TERMS - 2:
                copy = pltpu.make_async_copy(tb.at[t % 2, c], last_prev.at[:, columns(c)], out_sem.at[c, 3])
                copy.start()
                outs.append(copy)
            if t == TERMS - 1:
                for k, start in ((1, 0), (2, height - mid_at)):
                    copy = pltpu.make_async_copy(
                        tb.at[t % 2, c, pl.ds(start, mid_at)],
                        last_cur.at[pl.ds(start, mid_at), columns(c)], out_sem.at[c, k])
                    copy.start()
                    outs.append(copy)
        copies = sums(t)
        for copy in copies:
            copy.start()
        sent.append(copies)

    for t in range(TERMS):
        for copy in sent[t]:
            copy.wait()
        whole = mom[t, 0]
        for i in range(1, n):
            whole = whole + mom[t, i]
        for k in range(whole.shape[0]):
            mom_ref[t:t + 1, k * LANES:(k + 1) * LANES] = whole[k:k + 1, :]
    for copy in outs:
        copy.wait()


def local(hamiltonian_blocks, block_columns, probe, previous, current, orbital_weight):
    n = lax.axis_size("slab")
    rows, slots, w, _ = hamiltonian_blocks.shape
    height, cols = current.shape
    cc = min(CHUNK, cols)
    chunks = cols // cc
    vmem = pl.BlockSpec(memory_space=pltpu.VMEM)
    hbm = pl.BlockSpec(memory_space=pl.ANY)
    bf16, f32 = jnp.bfloat16, jnp.float32
    return pl.pallas_call(
        functools.partial(kernel, n),
        out_shape=(
            jax.ShapeDtypeStruct((height, cols), f32),
            jax.ShapeDtypeStruct((height, cols), f32),
            jax.ShapeDtypeStruct((TERMS, cols), f32),
        ),
        in_specs=[pl.BlockSpec(memory_space=pltpu.SMEM), vmem, hbm, hbm, hbm, hbm],
        out_specs=(hbm, hbm, vmem),
        scratch_shapes=[
            pltpu.VMEM((rows, slots, w, w), bf16),
            pltpu.VMEM((rows // GROUP, GROUP * w, (GROUP + 2 * BAND) * w), bf16),
            pltpu.VMEM((TERMS, chunks, height + 2 * BAND * w, cc), bf16),
            pltpu.VMEM((2, chunks, height, cc), f32),
            pltpu.VMEM((chunks, height, cc), f32),
            pltpu.VMEM((height, cols), bf16),
            pltpu.VMEM((TERMS, n, cols // LANES, LANES), f32),
            pltpu.SemaphoreType.DMA((4 * chunks + 2,)),
            pltpu.SemaphoreType.DMA((chunks, 4)),
            pltpu.SemaphoreType.DMA((TERMS, chunks, 2)),
            pltpu.SemaphoreType.DMA((TERMS, chunks, 2)),
            pltpu.SemaphoreType.DMA((TERMS, n)),
            pltpu.SemaphoreType.DMA((TERMS, n)),
        ],
        compiler_params=pltpu.CompilerParams(
            collective_id=0, has_side_effects=True, vmem_limit_bytes=48 * 1024 * 1024,
        ),
    )(block_columns, orbital_weight.reshape(rows, w), hamiltonian_blocks, probe, previous, current)


def solution(mesh):
    return jax.shard_map(
        local,
        mesh=mesh,
        in_specs=(
            P("slab", None, None, None),
            P("slab", None),
            P("slab", "col"),
            P("slab", "col"),
            P("slab", "col"),
            P("slab"),
        ),
        out_specs=(P("slab", "col"), P("slab", "col"), P(None, "col")),
        check_vma=False,
    )
```

profile of v0, /device:TPU:0, one launch (start us, length us, event | category | flops | bytes accessed | tf_op | source)
XLA Modules:
  0.0 65.8 jit_solution(13389513180402258276)
XLA Ops:
  0.6 0.0 copy-start
  0.6 1.6 %copy-done = bf16[2048,512]{1,0:T(8,128)(2,1)S(1)} copy-done((bf16[2048,512]{1,0:T(8,128)(2,1)S(1)}, bf16[2048,512]{1,0:T(8,128)(2,1)}, u32[]{:S(2)}) %copy-start) | copy-done | bytes 2097176
  2.2 0.0 copy-start.1
  2.2 0.7 %copy-done.1 = s32[16,9]{1,0:T(8,128)S(1)} copy-done((s32[16,9]{1,0:T(8,128)S(1)}, s32[16,9]{1,0:T(8,128)}, u32[]{:S(2)}) %copy-start.1) | copy-done | bytes 600
  2.9 0.0 copy-start.2
  2.9 0.7 %copy-done.2 = f32[2048]{0:T(1024)S(1)} copy-done((f32[2048]{0:T(1024)S(1)}, f32[2048]{0:T(1024)}, u32[]{:S(2)}) %copy-start.2) | copy-done | bytes 8216
  3.6 54.7 %shard_map.85 = (f32[2048,512]{1,0:T(8,128)}, f32[2048,512]{1,0:T(8,128)}, f32[3,512]{1,0:T(4,128)S(1)}) custom-call(s32[16,9]{1,0:T(8,128)S(1)} %copy-done.1, f32[16,128]{1,0:T(8,128)S(1)} %bitcast.1, bf16[16,9,128,128]{3,2,1,0:T(8,128)(2,1)} %h_hbm.1, bf16[2048,512]{1,0:T(8,128)(2,1)S(1)} %copy-done, f32[2048,512]{1,0:T(8,128)} %prev_hbm.1, ...), custom_call_target="tpu_custom_call" | custom-call | tf_op jit(solution)/shard_map/pallas_call | solution.py:236
  58.3 0.0 copy-start.3
  58.4 4.8 %copy.12 = f32[2048,512]{1,0:T(8,128)} copy(f32[2048,512]{1,0:T(8,128)} %get-tuple-element.6) | data formatting | bytes 8388608
  63.2 0.0 copy-done.3
  63.2 2.0 %copy.13 = f32[2048,512]{1,0:T(8,128)} copy(f32[2048,512]{1,0:T(8,128)S(1)} %copy-done.3) | data formatting | bytes 8388608
  65.2 0.6 copy.14
Async XLA Ops:
  0.6 1.6 %copy-start = (bf16[2048,512]{1,0:T(8,128)(2,1)S(1)}, bf16[2048,512]{1,0:T(8,128)(2,1)}, u32[]{:S(2)}) copy-start(bf16[2048,512]{1,0:T(8,128)(2,1)} %probe_hbm.1) | copy-start | bytes 6291460
  2.2 0.7 %copy-start.1 = (s32[16,9]{1,0:T(8,128)S(1)}, s32[16,9]{1,0:T(8,128)}, u32[]{:S(2)}) copy-start(s32[16,9]{1,0:T(8,128)} %col_ref.1) | copy-start | bytes 1732
  2.9 0.7 %copy-start.2 = (f32[2048]{0:T(1024)S(1)}, f32[2048]{0:T(1024)}, u32[]{:S(2)}) copy-start(f32[2048]{0:T(1024)} %param.11) | copy-start | bytes 24580
  58.3 4.8 %copy-start.3 = (f32[2048,512]{1,0:T(8,128)S(1)}, f32[2048,512]{1,0:T(8,128)}, u32[]{:S(2)}) copy-start(f32[2048,512]{1,0:T(8,128)} %get-tuple-element.7) | copy-start | bytes 12582916
where the time goes:
time: 66 us; the launch traced here: 65.8 us
  Pallas kernels  54.7 us (83%)
  local copies, waits for them, and re-layouts  10.4 us (16%)
  between operations  0.66 us (1%)
    pallas_call x1, Pallas kernels, local(): pl.pallas_call(functools.partial(kernel, n), out_shape=(jax.ShapeDtypeStr...  54.7 us
    unnamed x11, local copies, waits for them, and re-layouts  10.4 us

commit v1 on v0

v1 whole, which is shorter than its diff:
```python
import functools

import jax
import jax.numpy as jnp
from jax import lax
from jax.experimental import pallas as pl
from jax.experimental.pallas import tpu as pltpu
from jax.sharding import PartitionSpec as P

BAND = 5
TERMS = 3
LANES = 128
CHUNK = 256
GROUP = 2


def kernel(
    n, col_hbm, ow_hbm, h_hbm, probe_hbm, prev_hbm, cur_hbm,
    tb, mom,
    col_ref, ow_ref, hv, hb, ext, wts, pv,
    in_sem, send_sem, recv_sem, msend, mrecv,
):
    me = lax.axis_index("slab")
    rows, slots, w, _ = hv.shape
    chunks, height, cc = wts.shape
    total = n * rows
    rim = BAND * w
    gw = GROUP * w
    pairs = rows // GROUP
    edge = -(-BAND // GROUP)
    depth = gw + 2 * rim
    first = me * rows
    far = lax.rem(me, 2)
    near = 1 - far

    def columns(c):
        return pl.ds(c * cc, cc)

    def rim_in(c, side):
        start = pl.multiple_of(side * (height - rim), w)
        return pltpu.make_async_copy(
            cur_hbm.at[pl.ds(start, rim), columns(c)],
            tb.at[1, c, pl.ds(start, rim)],
            in_sem.at[3 * c + side],
        )

    inner = height - 2 * rim
    inner_in = [
        pltpu.make_async_copy(
            cur_hbm.at[pl.ds(rim, inner), columns(c)], tb.at[1, c, pl.ds(rim, inner)],
            in_sem.at[3 * c + 2])
        for c in range(chunks)
    ]
    base = 3 * chunks
    h_in = pltpu.make_async_copy(h_hbm, hv, in_sem.at[base])
    probe_in = pltpu.make_async_copy(probe_hbm, pv, in_sem.at[base + 1])
    col_in = pltpu.make_async_copy(col_hbm, col_ref, in_sem.at[base + 2])
    ow_in = pltpu.make_async_copy(ow_hbm, ow_ref, in_sem.at[base + 3])
    prev_in = [
        pltpu.make_async_copy(prev_hbm.at[:, columns(c)], tb.at[0, c], in_sem.at[base + 4 + c])
        for c in range(chunks)
    ]
    for c in range(chunks):
        rim_in(c, far).start()
        rim_in(c, near).start()

    barrier = pltpu.get_barrier_semaphore()
    for k in range(1, n):
        pl.semaphore_signal(
            barrier, inc=1, device_id={"slab": lax.rem(me + k, n)},
            device_id_type=pl.DeviceIdType.MESH,
        )

    def halo(t, c, side):
        source = pl.multiple_of(rim + side * (height - rim), w)
        target = pl.multiple_of((1 - side) * (rim + height), w)
        return pltpu.make_async_remote_copy(
            src_ref=ext.at[t, c, pl.ds(source, rim)],
            dst_ref=ext.at[t, c, pl.ds(target, rim)],
            send_sem=send_sem.at[t, c, side], recv_sem=recv_sem.at[t, c, 1 - side],
            device_id={"slab": lax.rem(me + n - 1 + 2 * side, n)},
            device_id_type=pl.DeviceIdType.MESH,
        )

    def cast(c, start, steps):
        def body(i, carry):
            at = pl.multiple_of(start + i * w, w)
            ext[0, c, pl.ds(pl.multiple_of(rim + at, w), w)] = tb[1, c, pl.ds(at, w)].astype(jnp.bfloat16)
            return carry

        lax.fori_loop(0, steps, body, 0)

    for c in range(chunks):
        for side in (far, near):
            rim_in(c, side).wait()
            cast(c, side * (height - rim), BAND)
            if c == 0 and side is far:
                for copy in inner_in:
                    copy.start()
                col_in.start()
                h_in.start()
                ow_in.start()
                probe_in.start()
                for copy in prev_in:
                    copy.start()
                pl.semaphore_wait(barrier, n - 1)
            halo(0, c, side).start()
    for c in range(chunks):
        inner_in[c].wait()
        cast(c, rim, inner // w)

    col_in.wait()
    h_in.wait()
    zero = jnp.zeros((w, w), jnp.bfloat16)

    def build(p, carry):
        for half in range(GROUP):
            r = p * GROUP + half
            places = []
            for s in range(slots):
                x = col_ref[r, s] - (first + r) + BAND
                x = jnp.where(x < 0, x + total, x)
                places.append(jnp.where(x >= total, x - total, x))
            for d in range(GROUP + 2 * BAND):
                place = d - half
                if place < 0 or place > 2 * BAND:
                    block = zero
                else:
                    slot = jnp.int32(0)
                    hit = jnp.int32(0)
                    for s in range(slots):
                        same = places[s] == place
                        slot = jnp.where(same, s, slot)
                        hit = jnp.where(same, 1, hit)
                    block = jnp.where(hit == 1, hv[r, slot], zero)
                hb[p, half * w:(half + 1) * w, d * w:(d + 1) * w] = block
        return carry

    lax.fori_loop(0, pairs, build, 0)

    probe_in.wait()
    ow_in.wait()
    eye = lax.broadcasted_iota(jnp.int32, (w, w), 0) == lax.broadcasted_iota(jnp.int32, (w, w), 1)

    def weigh(r, carry):
        row = jnp.broadcast_to(ow_ref[pl.ds(r, 1), :], (w, w))
        column = jnp.sum(jnp.where(eye, row, 0.0), axis=1, keepdims=True) / (total * w)
        at = pl.multiple_of(r * w, w)
        for c in range(chunks):
            wts[c, pl.ds(at, w)] = column * pv[pl.ds(at, w), c * cc:(c + 1) * cc].astype(jnp.float32)
        return carry

    lax.fori_loop(0, rows, weigh, 0)
    for copy in prev_in:
        copy.wait()

    def tile(t, c, p, acc):
        at = pl.multiple_of(p * gw, gw)
        product = jnp.dot(hb[p], ext[t, c, pl.ds(at, depth)], preferred_element_type=jnp.float32)
        upcoming = 2.0 * product - tb[t % 2, c, pl.ds(at, gw)]
        tb[t % 2, c, pl.ds(at, gw)] = upcoming
        if t + 1 < TERMS:
            ext[t + 1, c, pl.ds(pl.multiple_of(rim + at, w), gw)] = upcoming.astype(jnp.bfloat16)
        y = wts[c, pl.ds(at, gw)] * upcoming
        return acc + jnp.sum(y.reshape(gw // 8, 8, cc), axis=0)

    def sums(t):
        return [
            pltpu.make_async_remote_copy(
                src_ref=mom.at[t, me], dst_ref=mom.at[t, me],
                send_sem=msend.at[t, k], recv_sem=mrecv.at[t, k],
                device_id={"slab": lax.rem(me + k, n)}, device_id_type=pl.DeviceIdType.MESH,
            )
            for k in range(1, n)
        ]

    sent = []
    for t in range(TERMS):
        for c in range(chunks):
            acc = jnp.zeros((8, cc), jnp.float32)
            acc = lax.fori_loop(edge, pairs - edge, lambda p, a: tile(t, c, p, a), acc)
            for side in (near, far):
                halo(t, c, 1 - side).wait_recv()
                acc = lax.fori_loop(
                    0, edge, lambda i, a: tile(t, c, i + side * (pairs - edge), a), acc)
                if t + 1 < TERMS:
                    halo(t + 1, c, side).start()
            total_row = jnp.sum(acc, axis=0, keepdims=True)
            for k in range(cc // LANES):
                mom[t, me, pl.ds(c * (cc // LANES) + k, 1), :] = total_row[:, k * LANES:(k + 1) * LANES]
        copies = sums(t)
        for copy in copies:
            copy.start()
        sent.append(copies)

    for t in range(TERMS):
        for c in range(chunks):
            for side in (near, far):
                halo(t, c, side).wait_send()
    for copies in sent:
        for copy in copies:
            copy.wait()


def finish(tb, mom, last_prev, last_cur, mom_hbm, row_sums, sem):
    terms, n, lanes_of, _ = mom.shape
    _, chunks, _, cc = tb.shape
    copies = []
    for c in range(chunks):
        for k, out in enumerate((last_cur, last_prev)):
            source = (terms - 1 + k) % 2
            copies.append(pltpu.make_async_copy(
                tb.at[source, c], out.at[:, pl.ds(c * cc, cc)], sem.at[2 * c + k]))
    for copy in copies:
        copy.start()
    for t in range(terms):
        whole = mom[t, 0]
        for i in range(1, n):
            whole = whole + mom[t, i]
        for k in range(lanes_of):
            row_sums[t:t + 1, k * LANES:(k + 1) * LANES] = whole[k:k + 1, :]
    copies.append(pltpu.make_async_copy(row_sums, mom_hbm, sem.at[2 * chunks]))
    copies[-1].start()
    for copy in copies:
        copy.wait()


def local(hamiltonian_blocks, block_columns, probe, previous, current, orbital_weight):
    n = lax.axis_size("slab")
    rows, slots, w, _ = hamiltonian_blocks.shape
    height, cols = current.shape
    cc = min(CHUNK, cols)
    chunks = cols // cc
    vmem = pl.BlockSpec(memory_space=pltpu.VMEM)
    hbm = pl.BlockSpec(memory_space=pltpu.HBM)
    bf16, f32 = jnp.bfloat16, jnp.float32
    tb, mom = pl.pallas_call(
        functools.partial(kernel, n),
        out_shape=(
            pltpu.VMEM((2, chunks, height, cc), f32),
            pltpu.VMEM((TERMS, n, cols // LANES, LANES), f32),
        ),
        in_specs=[hbm] * 6,
        out_specs=(vmem, vmem),
        scratch_shapes=[
            pltpu.SMEM((rows, slots), jnp.int32),
            pltpu.VMEM((rows, w), f32),
            pltpu.VMEM((rows, slots, w, w), bf16),
            pltpu.VMEM((rows // GROUP, GROUP * w, (GROUP + 2 * BAND) * w), bf16),
            pltpu.VMEM((TERMS, chunks, height + 2 * BAND * w, cc), bf16),
            pltpu.VMEM((chunks, height, cc), f32),
            pltpu.VMEM((height, cols), bf16),
            pltpu.SemaphoreType.DMA((4 * chunks + 4,)),
            pltpu.SemaphoreType.DMA((TERMS, chunks, 2)),
            pltpu.SemaphoreType.DMA((TERMS, chunks, 2)),
            pltpu.SemaphoreType.DMA((TERMS, n)),
            pltpu.SemaphoreType.DMA((TERMS, n)),
        ],
        compiler_params=pltpu.CompilerParams(
            collective_id=0, has_side_effects=True, vmem_limit_bytes=44 * 1024 * 1024,
        ),
    )(block_columns, orbital_weight.reshape(rows, w), hamiltonian_blocks, probe, previous, current)
    return pl.pallas_call(
        finish,
        out_shape=(
            jax.ShapeDtypeStruct((height, cols), f32),
            jax.ShapeDtypeStruct((height, cols), f32),
            jax.ShapeDtypeStruct((TERMS, cols), f32),
        ),
        in_specs=[vmem, vmem],
        out_specs=(hbm, hbm, hbm),
        scratch_shapes=[
            pltpu.VMEM((TERMS, cols), f32),
            pltpu.SemaphoreType.DMA((2 * chunks + 1,)),
        ],
        compiler_params=pltpu.CompilerParams(vmem_limit_bytes=16 * 1024 * 1024),
    )(tb, mom)


def solution(mesh):
    return jax.shard_map(
        local,
        mesh=mesh,
        in_specs=(
            P("slab", None, None, None),
            P("slab", None),
            P("slab", "col"),
            P("slab", "col"),
            P("slab", "col"),
            P("slab"),
        ),
        out_specs=(P("slab", "col"), P("slab", "col"), P(None, "col")),
        check_vma=False,
    )
```

time: 66 us -> 58.5 us (0.89)
  local copies, waits for them, and re-layouts: 10.4 us -> 1.39 us
  Pallas kernels: 54.7 us -> 56.2 us
    unnamed x11 -> x4, local copies, waits for them, and re-layouts: 10.4 us -> 1.39 us
    pallas_call x1 -> x2, Pallas kernels: 54.7 us -> 56.2 us  [the longest x1 52.8 us: local(): pl.pallas_call(functools.partial(kernel, n), out_shape=(pltpu.VMEM((2, ch...]
where the time goes in v1:
time: 58.5 us; the launch traced here: 58.2 us
  Pallas kernels  56.2 us (96%)
  local copies, waits for them, and re-layouts  1.39 us (2%)
  between operations  0.65 us (1%)
    pallas_call x1, Pallas kernels, local(): pl.pallas_call(functools.partial(kernel, n), out_shape=(pltpu.VMEM((2, ch...  52.8 us
    pallas_call x1, Pallas kernels, local(): pl.pallas_call(finish, out_shape=(jax.ShapeDtypeStruct((height, cols), f3...  3.38 us
    unnamed x4, local copies, waits for them, and re-layouts  1.39 us

profile of v1, /device:TPU:0, one launch (start us, length us, event | category | flops | bytes accessed | tf_op | source)
XLA Modules:
  0.0 58.2 jit_solution(5582810214088908706)
XLA Ops:
  0.6 0.0 copy-start
  0.6 0.7 %copy-done = s32[16,9]{1,0:T(8,128)S(1)} copy-done((s32[16,9]{1,0:T(8,128)S(1)}, s32[16,9]{1,0:T(8,128)}, u32[]{:S(2)}) %copy-start) | copy-done | bytes 600
  1.3 0.0 copy-start.1
  1.3 0.7 %copy-done.1 = f32[2048]{0:T(1024)S(1)} copy-done((f32[2048]{0:T(1024)S(1)}, f32[2048]{0:T(1024)}, u32[]{:S(2)}) %copy-start.1) | copy-done | bytes 8216
  2.0 52.8 %shard_map.85 = (f32[2,2,2048,256]{3,2,1,0:T(8,128)S(1)}, f32[3,8,4,128]{3,2,1,0:T(4,128)S(1)}) custom-call(s32[16,9]{1,0:T(8,128)S(1)} %copy-done, f32[16,128]{1,0:T(8,128)S(1)} %bitcast.1, bf16[16,9,128,128]{3,2,1,0:T(8,128)(2,1)} %h_hbm.1, bf16[2048,512]{1,0:T(8,128)(2,1)} %probe_hbm.1, f32[2048,512]{1,0:T(8,128)} %prev_hbm.1, f32[2048,512]{1,0:T(8,128)} %cur_hbm.1), custom_call_target="tpu_custom_call" | custom-call | tf_op jit(solution)/shard_map/pallas_call | solution.py:237
  54.8 3.4 %shard_map.86 = (f32[2048,512]{1,0:T(8,128)}, f32[2048,512]{1,0:T(8,128)}, f32[3,512]{1,0:T(4,128)}) custom-call(f32[2,2,2048,256]{3,2,1,0:T(8,128)S(1)} %get-tuple-element.5.tb, f32[3,8,4,128]{3,2,1,0:T(4,128)S(1)} %get-tuple-element.6.mom), custom_call_target="tpu_custom_call" | custom-call | tf_op jit(solution)/shard_map/pallas_call | solution.py:263
Async XLA Ops:
  0.6 0.7 %copy-start = (s32[16,9]{1,0:T(8,128)S(1)}, s32[16,9]{1,0:T(8,128)}, u32[]{:S(2)}) copy-start(s32[16,9]{1,0:T(8,128)} %col_hbm.1) | copy-start | bytes 1732
  1.3 0.7 %copy-start.1 = (f32[2048]{0:T(1024)S(1)}, f32[2048]{0:T(1024)}, u32[]{:S(2)}) copy-start(f32[2048]{0:T(1024)} %param.11) | copy-start | bytes 24580

commit v2 on v1

--- a/solution.py
+++ b/solution.py
@@ -71,13 +71,17 @@
             device_id_type=pl.DeviceIdType.MESH,
         )
 
-    def halo(t, c, side):
-        source = pl.multiple_of(rim + side * (height - rim), w)
-        target = pl.multiple_of((1 - side) * (rim + height), w)
+    inside = BAND - GROUP
+
+    def halo(t, c, side, part):
+        size = (BAND - inside if part else inside) * w
+        offset = (1 - side) * inside * w if part else side * (BAND - inside) * w
+        source = pl.multiple_of(rim + side * (height - rim) + offset, w)
+        target = pl.multiple_of((1 - side) * (rim + height) + offset, w)
         return pltpu.make_async_remote_copy(
-            src_ref=ext.at[t, c, pl.ds(source, rim)],
-            dst_ref=ext.at[t, c, pl.ds(target, rim)],
-            send_sem=send_sem.at[t, c, side], recv_sem=recv_sem.at[t, c, 1 - side],
+            src_ref=ext.at[t, c, pl.ds(source, size)],
+            dst_ref=ext.at[t, c, pl.ds(target, size)],
+            send_sem=send_sem.at[t, c, side, part], recv_sem=recv_sem.at[t, c, 1 - side, part],
             device_id={"slab": lax.rem(me + n - 1 + 2 * side, n)},
             device_id_type=pl.DeviceIdType.MESH,
         )
@@ -104,7 +108,8 @@
                 for copy in prev_in:
                     copy.start()
                 pl.semaphore_wait(barrier, n - 1)
-            halo(0, c, side).start()
+            for part in range(2):
+                halo(0, c, side, part).start()
     for c in range(chunks):
         inner_in[c].wait()
         cast(c, rim, inner // w)
@@ -180,11 +185,16 @@
             acc = jnp.zeros((8, cc), jnp.float32)
             acc = lax.fori_loop(edge, pairs - edge, lambda p, a: tile(t, c, p, a), acc)
             for side in (near, far):
-                halo(t, c, 1 - side).wait_recv()
-                acc = lax.fori_loop(
-                    0, edge, lambda i, a: tile(t, c, i + side * (pairs - edge), a), acc)
+                def rim_tile(i, a):
+                    return tile(t, c, (1 - side) * (edge - 1 - i) + side * (pairs - edge + i), a)
+
+                halo(t, c, 1 - side, 0).wait_recv()
+                acc = lax.fori_loop(0, edge - 1, rim_tile, acc)
+                halo(t, c, 1 - side, 1).wait_recv()
+                acc = rim_tile(edge - 1, acc)
                 if t + 1 < TERMS:
-                    halo(t + 1, c, side).start()
+                    for part in range(2):
+                        halo(t + 1, c, side, part).start()
             total_row = jnp.sum(acc, axis=0, keepdims=True)
             for k in range(cc // LANES):
                 mom[t, me, pl.ds(c * (cc // LANES) + k, 1), :] = total_row[:, k * LANES:(k + 1) * LANES]
@@ -196,7 +206,8 @@
     for t in range(TERMS):
         for c in range(chunks):
             for side in (near, far):
-                halo(t, c, side).wait_send()
+                for part in range(2):
+                    halo(t, c, side, part).wait_send()
     for copies in sent:
         for copy in copies:
             copy.wait()
@@ -234,6 +245,7 @@
     vmem = pl.BlockSpec(memory_space=pltpu.VMEM)
     hbm = pl.BlockSpec(memory_space=pltpu.HBM)
     bf16, f32 = jnp.bfloat16, jnp.float32
+    grant = 67043328 - 4 * (2 * height * cols + TERMS * n * cols) - (64 << 10)
     tb, mom = pl.pallas_call(
         functools.partial(kernel, n),
         out_shape=(
@@ -251,13 +263,13 @@
             pltpu.VMEM((chunks, height, cc), f32),
             pltpu.VMEM((height, cols), bf16),
             pltpu.SemaphoreType.DMA((4 * chunks + 4,)),
-            pltpu.SemaphoreType.DMA((TERMS, chunks, 2)),
-            pltpu.SemaphoreType.DMA((TERMS, chunks, 2)),
+            pltpu.SemaphoreType.DMA((TERMS, chunks, 2, 2)),
+            pltpu.SemaphoreType.DMA((TERMS, chunks, 2, 2)),
             pltpu.SemaphoreType.DMA((TERMS, n)),
             pltpu.SemaphoreType.DMA((TERMS, n)),
         ],
         compiler_params=pltpu.CompilerParams(
-            collective_id=0, has_side_effects=True, vmem_limit_bytes=44 * 1024 * 1024,
+            collective_id=0, has_side_effects=True, vmem_limit_bytes=grant,
         ),
     )(block_columns, orbital_weight.reshape(rows, w), hamiltonian_blocks, probe, previous, current)
     return pl.pallas_call(

time: 58.5 us -> 56.5 us (0.966)
  local copies, waits for them, and re-layouts: 1.39 us -> 0 us
    unnamed x4 -> x0, local copies, waits for them, and re-layouts: 1.39 us -> none
where the time goes in v2:
time: 56.5 us; the launch traced here: 56.3 us
  Pallas kernels  55.7 us (99%)
  between operations  0.64 us (1%)
    pallas_call x1, Pallas kernels, local(): pl.pallas_call(functools.partial(kernel, n), out_shape=(pltpu.VMEM((2, ch...  52.3 us
    pallas_call x1, Pallas kernels, local(): pl.pallas_call(finish, out_shape=(jax.ShapeDtypeStruct((height, cols), f3...  3.38 us

profile of v2, /device:TPU:0, one launch (start us, length us, event | category | flops | bytes accessed | tf_op | source)
XLA Modules:
  0.0 56.3 jit_solution(5583989961487576398)
XLA Ops:
  0.6 52.3 %shard_map.85 = (f32[2,2,2048,256]{3,2,1,0:T(8,128)S(1)}, f32[3,8,4,128]{3,2,1,0:T(4,128)S(1)}) custom-call(s32[16,9]{1,0:T(8,128)} %col_hbm.1, f32[16,128]{1,0:T(8,128)} %bitcast.1, bf16[16,9,128,128]{3,2,1,0:T(8,128)(2,1)} %h_hbm.1, bf16[2048,512]{1,0:T(8,128)(2,1)} %probe_hbm.1, f32[2048,512]{1,0:T(8,128)} %prev_hbm.1, f32[2048,512]{1,0:T(8,128)} %cur_hbm.1), custom_call_target="tpu_custom_call" | custom-call | tf_op jit(solution)/shard_map/pallas_call | solution.py:249
  53.0 3.4 %shard_map.86 = (f32[2048,512]{1,0:T(8,128)}, f32[2048,512]{1,0:T(8,128)}, f32[3,512]{1,0:T(4,128)}) custom-call(f32[2,2,2048,256]{3,2,1,0:T(8,128)S(1)} %get-tuple-element.5.tb, f32[3,8,4,128]{3,2,1,0:T(4,128)S(1)} %get-tuple-element.6.mom), custom_call_target="tpu_custom_call" | custom-call | tf_op jit(solution)/shard_map/pallas_call | solution.py:275
